TPU v7x, 128 devices: a whole 4x4x4 slice. The times are simulated.
128 devices in a mesh: fsdp: 16 (over z, x_lo, core), cols: 8 (over y, x_hi).
Axes of the slice: x: 4 (x_hi: 2, x_lo: 2; x = x_hi * 2 + x_lo), y: 4, z: 4, core: 2. Of those that a mesh axis runs over, the one named last changes fastest.
Arguments:
- weight_query: bfloat16 [5120, 5120], P('fsdp', 'cols'), may hold values from -0.078125 to 0.078125
- low_query: bfloat16 [5120, 32], P('fsdp'), may hold values from -0.078125 to 0.078125
- high_query: bfloat16 [32, 5120], P(None, 'cols'), may hold values from -1 to 1
- weight_key: bfloat16 [5120, 5120], P('fsdp', 'cols'), may hold values from -0.078125 to 0.078125
- low_key: bfloat16 [5120, 32], P('fsdp'), may hold values from -0.078125 to 0.078125
- high_key: bfloat16 [32, 5120], P(None, 'cols'), may hold values from -1 to 1
- weight_value: bfloat16 [5120, 5120], P('fsdp', 'cols'), may hold values from -0.078125 to 0.078125
- low_value: bfloat16 [5120, 32], P('fsdp'), may hold values from -0.078125 to 0.078125
- high_value: bfloat16 [32, 5120], P(None, 'cols'), may hold values from -1 to 1
- weight_mixed: bfloat16 [5120, 5120], P('cols', 'fsdp'), may hold values from -0.078125 to 0.078125
- low_mixed: bfloat16 [5120, 32], P('cols'), may hold values from -0.078125 to 0.078125
- high_mixed: bfloat16 [32, 5120], P(None, 'fsdp'), may hold values from -1 to 1
- norm_train: float32 [5120], P(('fsdp', 'cols')), may hold values from 0.25 to 1.75
- norm_step: float32 [5120], P(('fsdp', 'cols')), may hold values from -0.3 to 0.3
Outputs:
- ready_query: bfloat16 [5120, 5120], P(None, 'cols')
- ready_key: bfloat16 [5120, 5120], P(None, 'cols')
- ready_value: bfloat16 [5120, 5120], P(None, 'cols')
- ready_mixed: bfloat16 [5120, 5120], P('cols')
- serve_norm: bfloat16 [5120], replicated
All inputs are finite; a program needn't handle non-finite values.
Results may differ from a plain program's by a relative error of at most 0.001.
Values may be sent and summed in bfloat16 or wider, within the bound.
No kernel may reach another device: no remote copies, remote signals or barrier semaphores. Data moves between devices by JAX's collectives and lax.ppermute only.
A program may use at most 192 MiB of HBM per device.

v0:
```python
import jax
import jax.numpy as jnp
from jax import lax
from jax.sharding import PartitionSpec as P

mix_rate = 2.0


def rows_first(arrays, axis, dims):
    turned = [jnp.moveaxis(a, dim, 0) for a, dim in zip(arrays, dims)]
    widths = [t[0].size for t in turned]
    both = jnp.concatenate([t.reshape(-1, w) for t, w in zip(turned, widths)], axis=1)
    result = lax.all_gather(both, axis, axis=0, tiled=True)
    blocks = jnp.split(result, [sum(widths[:k]) for k in range(1, len(widths))], axis=1)
    return tuple(
        (
            jnp.moveaxis(b.reshape(-1, *t.shape[1:]), 0, dim)
            for b, t, dim in zip(blocks, turned, dims)
        )
    )


def per_device(
    weight_query,
    low_query,
    high_query,
    weight_key,
    low_key,
    high_key,
    weight_value,
    low_value,
    high_value,
    weight_mixed,
    low_mixed,
    high_mixed,
    norm_train,
    norm_step,
):
    latest_query = weight_query.astype(jnp.float32) + mix_rate * jnp.dot(
        low_query, high_query, preferred_element_type=jnp.float32
    )
    latest_key = weight_key.astype(jnp.float32) + mix_rate * jnp.dot(
        low_key, high_key, preferred_element_type=jnp.float32
    )
    latest_value = weight_value.astype(jnp.float32) + mix_rate * jnp.dot(
        low_value, high_value, preferred_element_type=jnp.float32
    )
    latest_mixed = weight_mixed.astype(jnp.float32) + mix_rate * jnp.dot(
        low_mixed, high_mixed, preferred_element_type=jnp.float32
    )
    narrow_query, narrow_key, narrow_value, narrow_mixed = (
        latest_query.astype(jnp.bfloat16),
        latest_key.astype(jnp.bfloat16),
        latest_value.astype(jnp.bfloat16),
        latest_mixed.astype(jnp.bfloat16),
    )
    ready_query, ready_key, ready_value, ready_mixed = rows_first(
        (narrow_query, narrow_key, narrow_value, narrow_mixed), "fsdp", (0, 0, 0, 1)
    )
    serve_norm = lax.all_gather(
        (norm_train + norm_step).astype(jnp.bfloat16), ("fsdp", "cols"), axis=0, tiled=True
    )
    return (ready_query, ready_key, ready_value, ready_mixed, serve_norm)


def solution(mesh):
    in_specs = (
        P("fsdp", "cols"),
        P("fsdp", None),
        P(None, "cols"),
        P("fsdp", "cols"),
        P("fsdp", None),
        P(None, "cols"),
        P("fsdp", "cols"),
        P("fsdp", None),
        P(None, "cols"),
        P("cols", "fsdp"),
        P("cols", None),
        P(None, "fsdp"),
        P(("fsdp", "cols")),
        P(("fsdp", "cols")),
    )
    out_specs = (P(None, "cols"), P(None, "cols"), P(None, "cols"), P("cols", None), P())
    return jax.shard_map(
        per_device, mesh=mesh, in_specs=in_specs, out_specs=out_specs, check_vma=False
    )
```

profile of v0, /device:TPU:1, one launch (start us, length us, event | category | flops | bytes accessed | tf_op | source)
XLA Modules:
  0.0 190.2 jit_solution(9804116227767435953)
XLA Ops:
  7.2 0.0 copy-start
  7.2 0.0 all-gather.2.cloned.1.call-start
  7.2 0.7 copy-done
  8.0 1.3 fusion.4
  9.3 1.3 fusion.5
  10.6 0.0 copy-start.1
  10.6 0.0 copy-start.2
  10.6 1.3 fusion.6
  12.0 1.4 fusion.8
  13.4 1.3 pad_maximum_fusion
  14.7 0.0 all-gather.2.cloned.1.call-update
  14.7 0.0 copy-done.1
  14.7 0.0 copy-done.2
  14.7 0.2 dynamic-update-slice
  15.0 68.9 %all-reduce = bf16[5120]{0:T(1024)(128)(2,1)} all-reduce(bf16[5120]{0:T(1024)(128)(2,1)S(1)} %dynamic-update-slice), channel_id=1, replica_groups=mesh['fsdp'=16,'cols'=8] {'fsdp','cols'}, use_global_device_ids=true, to_apply=%add | all-reduce | flops 5120 | bytes 20480
  83.9 71.9 %all-gather.2.cloned.1.call-done = bf16[5120,2560]{1,0:T(8,128)(2,1)} async-done(((bf16[320,2560]{1,0:T(8,128)(2,1)}), bf16[5120,2560]{1,0:T(8,128)(2,1)}) %all-gather.2.cloned.1.call-update) | async-done | bytes 26214416 | tf_op jit(solution)/shard_map/all_gather | solution.py:13
  155.7 18.1 %slice_bitcast_fusion = (bf16[640,5120]{0,1:T(8,128)(2,1)}, bf16[5120,640]{1,0:T(8,128)(2,1)}, bf16[5120,640]{1,0:T(8,128)(2,1)}, bf16[5120,640]{1,0:T(8,128)(2,1)}) fusion(bf16[5120,2560]{1,0:T(8,128)(2,1)} %all-gather.2.cloned.1.call-done), kind=kLoop, calls=%fused_computation | loop fusion | bytes 52428800 | tf_op jit(solution)/shard_map/transpose | solution.py:17
  173.8 9.5 %copy.19 = bf16[640,5120]{1,0:T(8,128)(2,1)} copy(bf16[640,5120]{0,1:T(8,128)(2,1)} %get-tuple-element.10) | data formatting | bytes 13107200
  (2 shorter events, 0.0 us)
Async XLA Ops:
  7.2 0.8 copy-start
  7.2 148.5 %all-gather.2.cloned.1.call-start = ((), (), s32[]{:S(2)}) async-start(), calls=%async_computation | async-start | bytes 27852800 | tf_op jit(solution)/shard_map/all_gather | solution.py:13
  10.6 4.1 %copy-start.1 = (f32[40]{0:T(128)S(1)}, f32[40]{0:T(128)}, u32[]{:S(2)}) copy-start(f32[40]{0:T(128)} %param.26) | copy-start | bytes 484
  10.6 4.1 %copy-start.2 = (f32[40]{0:T(128)S(1)}, f32[40]{0:T(128)}, u32[]{:S(2)}) copy-start(f32[40]{0:T(128)} %param.27) | copy-start | bytes 484
Sparse Core Ops, SparseCore 0:
  14.8 140.8 all-gather.1
where the time goes:
time: 191 us; the launch traced here: 190 us
  waiting for transfers between devices  71.9 us (38%)
  blocking collectives  68.9 us (36%)
  local copies, waits for them, and re-layouts  28.6 us (15%)
  between operations  14.1 us (7%)
  matrix products  5.36 us (3%)
    all_gather x1, waiting for transfers between devices, rows_first(): result = lax.all_gather(both, axis, axis=0, tiled=True)  71.9 us
    unnamed x1, blocking collectives  68.9 us
    transpose x1, local copies, waits for them, and re-layouts, rows_first(): jnp.moveaxis(b.reshape(-1, *t.shape[1:]), 0, dim)  18.1 us
    unnamed x9, local copies, waits for them, and re-layouts  10.5 us
  transfers between devices with their start and end apart: 1, of which 1 were waited for; matrix products, arithmetic and copies ran while one was open for 0% of the time, Pallas kernels for 0%

commit v1 on v0

--- a/solution.py
+++ b/solution.py
@@ -10,7 +10,9 @@
     turned = [jnp.moveaxis(a, dim, 0) for a, dim in zip(arrays, dims)]
     widths = [t[0].size for t in turned]
     both = jnp.concatenate([t.reshape(-1, w) for t, w in zip(turned, widths)], axis=1)
-    result = lax.all_gather(both, axis, axis=0, tiled=True)
+    result = jnp.concatenate(
+        lax.all_to_all(jnp.stack([both] * lax.axis_size(axis)), axis, 0, 0), axis=0
+    )
     blocks = jnp.split(result, [sum(widths[:k]) for k in range(1, len(widths))], axis=1)
     return tuple(
         (

time: 191 us -> 393 us (2.06)
  blocking collectives: 68.9 us -> 341 us
  waiting for transfers between devices: 71.9 us -> 0.01 us
  between operations: 14.1 us -> 0.7 us
  local copies, waits for them, and re-layouts: 28.6 us -> 37.6 us
  starting transfers between devices: 0.04 us -> 7.88 us
    unnamed x1, blocking collectives: 68.9 us -> 341 us
    all_gather x1 -> x0, waiting for transfers between devices: 71.9 us -> none  [rows_first(): result = lax.all_gather(both, axis, axis=0, tiled=True)]
    another operation x0 -> x1, local copies, waits for them, and re-layouts: none -> 8.9 us  [rows_first(): jnp.stack([both] * lax.axis_size(axis))]
    all_to_all x0 -> x1, starting transfers between devices: none -> 7.88 us  [rows_first(): lax.all_to_all(jnp.stack([both] * lax.axis_size(axis)), axis, 0, 0)]
    unnamed x9 -> x11, local copies, waits for them, and re-layouts: 10.5 us -> 10.6 us
  transfers between devices with their start and end apart: 1 -> 1, of which waited for: 1 -> 0; matrix products, arithmetic and copies ran while one was open for 0% -> 0% of each run, Pallas kernels for 0% -> 0%
where the time goes in v1:
time: 393 us
  blocking collectives  341 us (87%)
  local copies, waits for them, and re-layouts  37.6 us (10%)
  starting transfers between devices  7.88 us (2%)
  matrix products  5.36 us (1%)
    unnamed x1, blocking collectives  341 us
    transpose x1, local copies, waits for them, and re-layouts, rows_first(): jnp.moveaxis(b.reshape(-1, *t.shape[1:]), 0, dim)  18.1 us
    unnamed x11, local copies, waits for them, and re-layouts  10.6 us
    another operation x1, local copies, waits for them, and re-layouts, rows_first(): jnp.stack([both] * lax.axis_size(axis))  8.9 us
    all_to_all x1, starting transfers between devices, rows_first(): lax.all_to_all(jnp.stack([both] * lax.axis_size(axis)), axis, 0, 0)  7.88 us
  transfers between devices with their start and end apart: 1, of which 0 were waited for; matrix products, arithmetic and copies ran while one was open for 0% of the time, Pallas kernels for 0%

profile of v1, /device:TPU:1, one launch (start us, length us, event | category | flops | bytes accessed | tf_op | source)
XLA Modules:
  0.0 392.7 jit_solution(11650202632882592164)
XLA Ops:
  0.6 0.0 copy-start
  0.6 0.8 copy-done
  1.4 1.3 fusion.4
  2.7 1.3 fusion.5
  4.1 1.3 fusion.6
  5.4 1.4 fusion.8
  6.8 0.1 pad_maximum_fusion
  6.9 8.9 %stack.2 = bf16[16,320,2560]{2,1,0:T(8,128)(2,1)} broadcast(bf16[320,2560]{1,0:T(8,128)(2,1)S(1)} %pad_maximum_fusion), dimensions={1,2} | broadcast | bytes 27852800 | tf_op jit(solution)/shard_map/stack | solution.py:14
  15.8 0.0 copy-start.2
  15.8 0.0 copy-start.3
  15.8 7.9 %all-to-all-start = ((bf16[16,320,2560]{2,1,0:T(8,128)(2,1)}), bf16[16,320,2560]{2,1,0:T(8,128)(2,1)}, u32[]{:S(2)}, u32[]{:S(2)}) async-start(bf16[16,320,2560]{2,1,0:T(8,128)(2,1)} %stack.2), calls=%async_computation | async-start | bytes 52428800 | tf_op jit(solution)/shard_map/all_to_all | solution.py:14
  23.7 0.0 copy-done.2
  23.7 0.0 copy-done.3
  23.8 0.2 dynamic-update-slice
  24.0 341.1 %all-reduce = bf16[5120]{0:T(1024)(128)(2,1)} all-reduce(bf16[5120]{0:T(1024)(128)(2,1)S(1)} %dynamic-update-slice), channel_id=1, replica_groups=mesh['fsdp'=16,'cols'=8] {'fsdp','cols'}, use_global_device_ids=true, to_apply=%add | all-reduce | flops 5120 | bytes 20480
  365.1 0.0 all-to-all-done
  365.1 18.1 %slice_bitcast_fusion = (bf16[640,5120]{0,1:T(8,128)(2,1)}, bf16[5120,640]{1,0:T(8,128)(2,1)}, bf16[5120,640]{1,0:T(8,128)(2,1)}, bf16[5120,640]{1,0:T(8,128)(2,1)}) fusion(bf16[5120,2560]{1,0:T(8,128)(2,1)} %bitcast.1), kind=kLoop, calls=%fused_computation | loop fusion | bytes 52428800 | tf_op jit(solution)/shard_map/transpose | solution.py:19
  383.2 0.0 copy-start.1
  383.2 9.5 %copy.23 = bf16[640,5120]{1,0:T(8,128)(2,1)} copy(bf16[640,5120]{0,1:T(8,128)(2,1)} %get-tuple-element.15) | data formatting | bytes 13107200
  392.7 0.0 copy-done.1
  (2 shorter events, 0.0 us)
Async XLA Ops:
  0.6 0.8 copy-start
  15.8 7.9 %copy-start.2 = (f32[40]{0:T(128)S(1)}, f32[40]{0:T(128)}, u32[]{:S(2)}) copy-start(f32[40]{0:T(128)} %param.26) | copy-start | bytes 484
  15.8 7.9 %copy-start.3 = (f32[40]{0:T(128)S(1)}, f32[40]{0:T(128)}, u32[]{:S(2)}) copy-start(f32[40]{0:T(128)} %param.27) | copy-start | bytes 484
  15.8 349.3 %all-to-all-start = ((bf16[16,320,2560]{2,1,0:T(8,128)(2,1)}), bf16[16,320,2560]{2,1,0:T(8,128)(2,1)}, u32[]{:S(2)}, u32[]{:S(2)}) async-start(bf16[16,320,2560]{2,1,0:T(8,128)(2,1)} %stack.2), calls=%async_computation | async-start | bytes 52428800 | tf_op jit(solution)/shard_map/all_to_all | solution.py:14
  383.2 9.5 %copy-start.1 = (bf16[32,640]{1,0:T(8,128)(2,1)S(1)}, bf16[32,640]{1,0:T(8,128)(2,1)}, u32[]{:S(2)}) copy-start(bf16[32,640]{1,0:T(8,128)(2,1)} %param.16) | copy-start | bytes 122884
